TPU v7x, 32 devices: a whole 2x2x4 slice. The times are simulated.
32 devices in a mesh: row: 8 (over y, x, core), col: 4 (over z).
Axes of the slice: x: 2, y: 2, z: 4, core: 2. Of those that a mesh axis runs over, the one named last changes fastest.
Arguments:
- columns: float32 [4096, 8192], P('col', 'row'), may hold values from -64 to 64
- block_order: int32 [64], P('col'), may hold values from 0 to 63, as said below
Outputs:
- rotated: float32 [4096, 8192], P('col', 'row')
Inputs may be any that keep to these rules, and one draw needn't show every extreme that they name: block_order is a permutation of 0 .. 63 in which slots c * 16 to (c + 1) * 16 - 1 name blocks c * 16 to (c + 1) * 16 - 1.
All inputs are finite; a program needn't handle non-finite values.
Results may differ from a plain program's by a relative error of at most 0.00055.
Values sent between devices are 32-bit elements; how exact they have to be, the bound alone decides.
A program may use at most 64 MiB of HBM per device.

v0:
```python
import jax
import jax.numpy as jnp
from jax import lax
from jax.sharding import PartitionSpec as P

BLOCK = 64
STEPS = 4


def shifted(value, axis, steps):
    count = lax.axis_size(axis)
    leading, last = (max(0, -steps), min(count, count - steps))
    return lax.ppermute(value, axis, [(source, source + steps) for source in range(leading, last)])


def make_systems(cross_sum, col_norms):
    highest = lax.Precision.HIGHEST
    top_norms = col_norms[:, :BLOCK][:, :, None]
    bottom_norms = col_norms[:, BLOCK:][:, None, :]
    spread = bottom_norms - top_norms
    radius = jnp.sqrt(spread * spread + 4.0 * cross_sum * cross_sum)
    scale_term = (top_norms + bottom_norms) / BLOCK
    coupling = (
        2.0
        * cross_sum
        * spread
        / (
            spread * spread
            + 4.0 * cross_sum * cross_sum
            + jnp.abs(spread) * radius
            + scale_term * scale_term
        )
    )
    identity = jnp.eye(BLOCK, dtype=jnp.float32)
    left_system = identity + jnp.einsum("pij,pkj->pik", coupling, coupling, precision=highest)
    right_system = identity + jnp.einsum("pji,pjk->pik", coupling, coupling, precision=highest)
    identities = jnp.broadcast_to(identity, coupling.shape)
    upper_half = jnp.concatenate([identities, coupling], axis=2)
    lower_half = jnp.concatenate([-jnp.transpose(coupling, (0, 2, 1)), identities], axis=2)
    systems = jnp.concatenate([left_system, right_system], axis=0)
    targets = jnp.concatenate([upper_half, lower_half], axis=0)
    return (systems, targets)


def solve_systems(systems, targets):
    factors = jnp.linalg.cholesky(systems)

    def solve_one(factor, target):
        return jax.scipy.linalg.cho_solve((factor, True), target)

    return jax.vmap(solve_one)(factors, targets)


def finish_turn(targets, solved_all):
    highest = lax.Precision.HIGHEST
    pairs = targets.shape[0] // 2
    solved = jnp.concatenate([solved_all[:pairs], solved_all[pairs:]], axis=1)
    plus_skew = jnp.concatenate([targets[:pairs], targets[pairs:]], axis=1)
    return jnp.einsum("pij,pjk->pik", plus_skew, solved, precision=highest)


def cayley_turn(cross_sum, col_norms):
    systems, targets = make_systems(cross_sum, col_norms)
    total = systems.shape[0]
    groups = lax.axis_size("row")
    share = -(-total // groups)
    start = lax.axis_index("row") * share
    mine_systems = lax.dynamic_slice_in_dim(systems, start, share, 0)
    mine_targets = lax.dynamic_slice_in_dim(targets, start, share, 0)
    mine_solved = solve_systems(mine_systems, mine_targets)
    gathered = lax.all_gather(mine_solved, "row", axis=0, tiled=True)
    return finish_turn(targets, gathered)


def local(columns, block_order):
    highest = lax.Precision.HIGHEST
    width, length = columns.shape
    count = width // BLOCK
    position = lax.axis_index("col")
    last_index = lax.axis_size("col") - 1
    local_index = block_order - position * block_order.shape[0]
    blocks = jnp.take(columns.reshape(count, BLOCK, length), local_index, axis=0)
    blocks = blocks.reshape(count // 2, 2 * BLOCK, length)
    for sweep_step in range(STEPS):
        cross_part = jnp.einsum(
            "pim,pjm->pij", blocks[:, :BLOCK], blocks[:, BLOCK:], precision=highest
        )
        norm_part = jnp.sum(blocks * blocks, axis=2)
        cross_sum, col_norms = lax.psum((cross_part, norm_part), "row")
        turn_matrix = cayley_turn(cross_sum, col_norms)
        turned = jnp.einsum("pij,pim->pjm", turn_matrix, blocks, precision=highest)
        top_blocks = turned[:, :BLOCK]
        bottom_blocks = turned[:, BLOCK:]
        from_left = shifted(top_blocks[-1], "col", 1)
        from_right = shifted(bottom_blocks[0], "col", -1)
        first_top = jnp.where(position == 0, top_blocks[0], from_left)
        second_top = jnp.where(position == 0, bottom_blocks[0], top_blocks[0])
        new_tops = jnp.concatenate([first_top[None], second_top[None], top_blocks[1:-1]], axis=0)
        last_bottom = jnp.where(position == last_index, top_blocks[-1], from_right)
        new_bottoms = jnp.concatenate([bottom_blocks[1:], last_bottom[None]], axis=0)
        blocks = jnp.concatenate([new_tops, new_bottoms], axis=1)
    return blocks.reshape(width, length)


def solution(mesh):
    placed = (P("col", "row"), P("col"))
    return jax.shard_map(
        local, mesh=mesh, in_specs=placed, out_specs=P("col", "row"), check_vma=False
    )
```

profile of v0, /device:TPU:0, one launch (start us, length us, event | category | flops | bytes accessed | tf_op | source)
XLA Modules:
  0.0 517.0 jit_solution(15705440596389083100)
XLA Ops:
  7.5 5.0 gather_fusion
  22.7 15.1 %psum.57 = f32[8,128]{1,0:T(8,128)S(1)} all-reduce(f32[8,128]{1,0:T(8,128)S(1)} %reduce_sum.39), channel_id=1, replica_groups=mesh['row'=8,'col'=4] {'row'}, use_global_device_ids=true, to_apply=%region_2.3 | all-reduce | flops 1024 | bytes 8192 | tf_op jit(solution)/shard_map/psum | solution.py:89
  38.1 38.6 %all-reduce.5.cloned.1.call-done = f32[8,64,64]{1,2,0:T(8,128)} async-done(((f32[8,64,64]{1,2,0:T(8,128)}), f32[8,64,64]{1,2,0:T(8,128)}) %all-reduce.5.cloned.1.call-update) | async-done | bytes 131088 | tf_op jit(solution)/shard_map/psum | solution.py:89
  79.3 11.7 %custom-call.14 = f32[2,64,64]{2,1,0:T(8,128)S(1)} custom-call(f32[2,64,64]{2,1,0:T(8,128)S(1)} %fusion.135), custom_call_target="Cholesky" | custom-call | tf_op jit(solution)/shard_map/jit(cholesky)/cholesky | solution.py:46
  91.2 9.8 %custom-call.15 = f32[2,1,64,64]{2,3,1,0:T(8,128)S(1)} custom-call(f32[2,1,64,64]{3,2,1,0:T(8,128)S(1)} %select_bitcast_fusion.7), custom_call_target="InvertDiagBlocksLowerTriangular" | custom-call | tf_op jit(solution)/shard_map/vmap(jit(_cho_solve))/triangular_solve | solution.py:49
  101.7 9.8 %all_gather.12 = f32[16,64,128]{2,1,0:T(8,128)S(1)} all-gather(f32[2,64,128]{2,1,0:T(8,128)S(1)} %fusion.132), channel_id=1, replica_groups=mesh['row'=8,'col'=4] {'row'}, dimensions={0}, use_global_device_ids=true | all-gather | bytes 589824 | tf_op jit(solution)/shard_map/all_gather | solution.py:71
  112.8 4.1 fusion.167
  128.5 4.1 collective-permute-done.1
  137.4 12.1 %psum.59 = f32[8,128]{1,0:T(8,128)S(1)} all-reduce(f32[8,128]{1,0:T(8,128)S(1)} %multiply_reduce_fusion.2), channel_id=1, replica_groups=mesh['row'=8,'col'=4] {'row'}, use_global_device_ids=true, to_apply=%region_7.10 | all-reduce | flops 1024 | bytes 8192 | tf_op jit(solution)/shard_map/psum | solution.py:89
  149.8 52.5 %all-reduce.7.cloned.1.call-done = f32[8,64,64]{1,2,0:T(8,128)} async-done(((f32[8,64,64]{1,2,0:T(8,128)}), f32[8,64,64]{1,2,0:T(8,128)}) %all-reduce.7.cloned.1.call-update) | async-done | bytes 131088 | tf_op jit(solution)/shard_map/psum | solution.py:89
  207.1 12.5 %custom-call.16 = f32[2,64,64]{2,1,0:T(8,128)S(1)} custom-call(f32[2,64,64]{2,1,0:T(8,128)} %fusion.131), custom_call_target="Cholesky" | custom-call | tf_op jit(solution)/shard_map/jit(cholesky)/cholesky | solution.py:46
  220.4 10.6 %custom-call.17 = f32[2,1,64,64]{2,3,1,0:T(8,128)S(1)} custom-call(f32[2,1,64,64]{3,2,1,0:T(8,128)} %select_bitcast_fusion.6), custom_call_target="InvertDiagBlocksLowerTriangular" | custom-call | tf_op jit(solution)/shard_map/vmap(jit(_cho_solve))/triangular_solve | solution.py:49
  231.6 9.2 %all_gather.13 = f32[16,64,128]{2,1,0:T(8,128)S(1)} all-gather(f32[2,64,128]{2,1,0:T(8,128)S(1)} %fusion.128), channel_id=1, replica_groups=mesh['row'=8,'col'=4] {'row'}, dimensions={0}, use_global_device_ids=true | all-gather | bytes 589824 | tf_op jit(solution)/shard_map/all_gather | solution.py:71
  242.1 3.8 fusion.32
  251.2 4.2 collective-permute-done.2
  255.4 4.1 collective-permute-done.3
  263.3 12.0 %psum.61 = f32[8,128]{1,0:T(8,128)S(1)} all-reduce(f32[8,128]{1,0:T(8,128)S(1)} %multiply_reduce_fusion.1), channel_id=1, replica_groups=mesh['row'=8,'col'=4] {'row'}, use_global_device_ids=true, to_apply=%region_10.13 | all-reduce | flops 1024 | bytes 8192 | tf_op jit(solution)/shard_map/psum | solution.py:89
  275.5 52.7 %all-reduce.9.cloned.1.call-done = f32[8,64,64]{1,2,0:T(8,128)} async-done(((f32[8,64,64]{1,2,0:T(8,128)}), f32[8,64,64]{1,2,0:T(8,128)}) %all-reduce.9.cloned.1.call-update) | async-done | bytes 131088 | tf_op jit(solution)/shard_map/psum | solution.py:89
  333.0 12.5 %custom-call.18 = f32[2,64,64]{2,1,0:T(8,128)S(1)} custom-call(f32[2,64,64]{2,1,0:T(8,128)} %fusion.127), custom_call_target="Cholesky" | custom-call | tf_op jit(solution)/shard_map/jit(cholesky)/cholesky | solution.py:46
  346.4 10.6 %custom-call.19 = f32[2,1,64,64]{2,3,1,0:T(8,128)S(1)} custom-call(f32[2,1,64,64]{3,2,1,0:T(8,128)} %select_bitcast_fusion.5), custom_call_target="InvertDiagBlocksLowerTriangular" | custom-call | tf_op jit(solution)/shard_map/vmap(jit(_cho_solve))/triangular_solve | solution.py:49
  357.5 9.4 %all_gather.14 = f32[16,64,128]{2,1,0:T(8,128)S(1)} all-gather(f32[2,64,128]{2,1,0:T(8,128)S(1)} %fusion.124), channel_id=1, replica_groups=mesh['row'=8,'col'=4] {'row'}, dimensions={0}, use_global_device_ids=true | all-gather | bytes 589824 | tf_op jit(solution)/shard_map/all_gather | solution.py:71
  368.2 3.8 fusion.31
  377.2 4.4 collective-permute-done.4
  381.6 4.1 collective-permute-done.5
  389.2 12.3 %psum.63 = f32[8,128]{1,0:T(8,128)S(1)} all-reduce(f32[8,128]{1,0:T(8,128)S(1)} %multiply_reduce_fusion), channel_id=1, replica_groups=mesh['row'=8,'col'=4] {'row'}, use_global_device_ids=true, to_apply=%region_13.16 | all-reduce | flops 1024 | bytes 8192 | tf_op jit(solution)/shard_map/psum | solution.py:89
  401.6 52.8 %all-reduce.11.cloned.1.call-done = f32[8,64,64]{1,2,0:T(8,128)} async-done(((f32[8,64,64]{1,2,0:T(8,128)}), f32[8,64,64]{1,2,0:T(8,128)}) %all-reduce.11.cloned.1.call-update) | async-done | bytes 131088 | tf_op jit(solution)/shard_map/psum | solution.py:89
  456.9 11.7 %custom-call.20 = f32[2,64,64]{2,1,0:T(8,128)S(1)} custom-call(f32[2,64,64]{2,1,0:T(8,128)S(1)} %fusion.123), custom_call_target="Cholesky" | custom-call | tf_op jit(solution)/shard_map/jit(cholesky)/cholesky | solution.py:46
  468.9 9.8 %custom-call.21 = f32[2,1,64,64]{2,3,1,0:T(8,128)S(1)} custom-call(f32[2,1,64,64]{3,2,1,0:T(8,128)S(1)} %select_bitcast_fusion.4), custom_call_target="InvertDiagBlocksLowerTriangular" | custom-call | tf_op jit(solution)/shard_map/vmap(jit(_cho_solve))/triangular_solve | solution.py:49
  479.5 9.2 %all_gather.15 = f32[16,64,128]{2,1,0:T(8,128)S(1)} all-gather(f32[2,64,128]{2,1,0:T(8,128)S(1)} %fusion.120), channel_id=1, replica_groups=mesh['row'=8,'col'=4] {'row'}, dimensions={0}, use_global_device_ids=true | all-gather | bytes 589824 | tf_op jit(solution)/shard_map/all_gather | solution.py:71
  489.9 3.8 fusion.30
  498.7 4.5 collective-permute-done.6
  503.3 4.1 collective-permute-done.7
  (157 shorter events, 77.2 us)
Async XLA Ops:
  6.5 70.1 %all-reduce.5.cloned.1.call-start = ((), (), s32[]{:S(2)}) async-start(), calls=%async_computation | async-start | bytes 524288 | tf_op jit(solution)/shard_map/psum | solution.py:89
  15.0 1.9 copy-start
  19.8 182.5 %all-reduce.7.cloned.1.call-start = ((), (), s32[]{:S(2)}) async-start(), calls=%async_computation.1 | async-start | bytes 524288 | tf_op jit(solution)/shard_map/psum | solution.py:89
  101.1 11.7 %copy-start.1 = (f32[8,128,1024]{2,1,0:T(8,128)S(1)}, f32[8,128,1024]{2,1,0:T(8,128)}, u32[]{:S(2)}) copy-start(f32[8,128,1024]{2,1,0:T(8,128)} %copy-done) | copy-start | bytes 12582916
  116.9 2.0 copy-start.2
  119.0 15.2 %copy-start.9 = (f32[1,64,1024]{2,1,0:T(8,128)}, f32[1,64,1024]{2,1,0:T(8,128)S(1)}, u32[]{:S(2)}) copy-start(f32[1,64,1024]{2,1,0:T(8,128)S(1)} %get-tuple-element.35) | copy-start | bytes 786436
  119.0 9.5 %collective-permute-start = (f32[64,1024]{1,0:T(8,128)S(1)}, f32[64,1024]{1,0:T(8,128)S(1)}, u32[]{:S(2)}, u32[]{:S(2)}) collective-permute-start(f32[64,1024]{1,0:T(8,128)S(1)} %get-tuple-element.36), channel_id=1, source_target_pairs={{0,1},{1,2},{2,3},{4,5},{5,6},{6,7},{8,9},{9,10},{10,11},{12,13},{... | collective-permute-start | bytes 786440 | tf_op jit(solution)/shard_map/ppermute | solution.py:13
  122.4 10.2 %collective-permute-start.1 = (f32[64,1024]{1,0:T(8,128)S(1)}, f32[64,1024]{1,0:T(8,128)S(1)}, u32[]{:S(2)}, u32[]{:S(2)}) collective-permute-start(f32[64,1024]{1,0:T(8,128)S(1)} %get-tuple-element.34), channel_id=1, source_target_pairs={{1,0},{2,1},{3,2},{5,4},{6,5},{7,6},{9,8},{10,9},{11,10},{13,12},{... | collective-permute-start | bytes 786440 | tf_op jit(solution)/shard_map/ppermute | solution.py:13
  126.9 7.3 %copy-start.7 = (f32[6,64,1024]{2,1,0:T(8,128)}, f32[6,64,1024]{2,1,0:T(8,128)S(1)}, u32[]{:S(2)}) copy-start(f32[6,64,1024]{2,1,0:T(8,128)S(1)} %slice.213) | copy-start | bytes 4718596
  133.7 0.7 copy-start.17
  133.7 0.8 copy-start.19
  149.5 178.7 %all-reduce.9.cloned.1.call-start = ((), (), s32[]{:S(2)}) async-start(), calls=%async_computation.2 | async-start | bytes 524288 | tf_op jit(solution)/shard_map/psum | solution.py:89
  204.9 37.2 %copy-start.10 = (f32[1,64,1024]{2,1,0:T(8,128)S(1)}, f32[1,64,1024]{2,1,0:T(8,128)}, u32[]{:S(2)}) copy-start(f32[1,64,1024]{2,1,0:T(8,128)} %copy-done.9) | copy-start | bytes 786436
  204.9 37.1 %copy-start.18 = (f32[1,64,1024]{2,1,0:T(8,128)S(1)}, f32[1,64,1024]{2,1,0:T(8,128)}, u32[]{:S(2)}) copy-start(f32[1,64,1024]{2,1,0:T(8,128)} %copy-done.17) | copy-start | bytes 786436
  204.9 37.1 %copy-start.20 = (f32[1,64,1024]{2,1,0:T(8,128)S(1)}, f32[1,64,1024]{2,1,0:T(8,128)}, u32[]{:S(2)}) copy-start(f32[1,64,1024]{2,1,0:T(8,128)} %copy-done.19) | copy-start | bytes 786436
  231.0 11.0 %copy-start.8 = (f32[6,64,1024]{2,1,0:T(8,128)S(1)}, f32[6,64,1024]{2,1,0:T(8,128)}, u32[]{:S(2)}) copy-start(f32[6,64,1024]{2,1,0:T(8,128)} %copy-done.7) | copy-start | bytes 4718596
  246.0 14.2 %copy-start.11 = (f32[1,64,1024]{2,1,0:T(8,128)}, f32[1,64,1024]{2,1,0:T(8,128)S(1)}, u32[]{:S(2)}) copy-start(f32[1,64,1024]{2,1,0:T(8,128)S(1)} %get-tuple-element.30) | copy-start | bytes 786436
  246.0 9.5 %collective-permute-start.2 = (f32[64,1024]{1,0:T(8,128)S(1)}, f32[64,1024]{1,0:T(8,128)S(1)}, u32[]{:S(2)}, u32[]{:S(2)}) collective-permute-start(f32[64,1024]{1,0:T(8,128)S(1)} %get-tuple-element.31), channel_id=1, source_target_pairs={{0,1},{1,2},{2,3},{4,5},{5,6},{6,7},{8,9},{9,10},{10,11},{12,13},{... | collective-permute-start | bytes 786440 | tf_op jit(solution)/shard_map/ppermute | solution.py:13
  249.4 10.2 %collective-permute-start.3 = (f32[64,1024]{1,0:T(8,128)S(1)}, f32[64,1024]{1,0:T(8,128)S(1)}, u32[]{:S(2)}, u32[]{:S(2)}) collective-permute-start(f32[64,1024]{1,0:T(8,128)S(1)} %get-tuple-element.29), channel_id=1, source_target_pairs={{1,0},{2,1},{3,2},{5,4},{6,5},{7,6},{9,8},{10,9},{11,10},{13,12},{... | collective-permute-start | bytes 786440 | tf_op jit(solution)/shard_map/ppermute | solution.py:13
  251.2 8.9 %copy-start.5 = (f32[6,64,1024]{2,1,0:T(8,128)}, f32[6,64,1024]{2,1,0:T(8,128)S(1)}, u32[]{:S(2)}) copy-start(f32[6,64,1024]{2,1,0:T(8,128)S(1)} %slice.220) | copy-start | bytes 4718596
  259.6 0.8 copy-start.15
  275.4 179.0 %all-reduce.11.cloned.1.call-start = ((), (), s32[]{:S(2)}) async-start(), calls=%async_computation.3 | async-start | bytes 524288 | tf_op jit(solution)/shard_map/psum | solution.py:89
  330.8 37.4 %copy-start.12 = (f32[1,64,1024]{2,1,0:T(8,128)S(1)}, f32[1,64,1024]{2,1,0:T(8,128)}, u32[]{:S(2)}) copy-start(f32[1,64,1024]{2,1,0:T(8,128)} %copy-done.11) | copy-start | bytes 786436
  330.8 37.4 %copy-start.14 = (f32[1,64,1024]{2,1,0:T(8,128)S(1)}, f32[1,64,1024]{2,1,0:T(8,128)}, u32[]{:S(2)}) copy-start(f32[1,64,1024]{2,1,0:T(8,128)} %copy-done.13) | copy-start | bytes 786436
  330.8 37.4 %copy-start.16 = (f32[1,64,1024]{2,1,0:T(8,128)S(1)}, f32[1,64,1024]{2,1,0:T(8,128)}, u32[]{:S(2)}) copy-start(f32[1,64,1024]{2,1,0:T(8,128)} %copy-done.15) | copy-start | bytes 786436
  356.9 11.3 %copy-start.6 = (f32[6,64,1024]{2,1,0:T(8,128)S(1)}, f32[6,64,1024]{2,1,0:T(8,128)}, u32[]{:S(2)}) copy-start(f32[6,64,1024]{2,1,0:T(8,128)} %copy-done.5) | copy-start | bytes 4718596
  372.1 9.5 %collective-permute-start.4 = (f32[64,1024]{1,0:T(8,128)S(1)}, f32[64,1024]{1,0:T(8,128)S(1)}, u32[]{:S(2)}, u32[]{:S(2)}) collective-permute-start(f32[64,1024]{1,0:T(8,128)S(1)} %get-tuple-element.26), channel_id=1, source_target_pairs={{0,1},{1,2},{2,3},{4,5},{5,6},{6,7},{8,9},{9,10},{10,11},{12,13},{... | collective-permute-start | bytes 786440 | tf_op jit(solution)/shard_map/ppermute | solution.py:13
  375.5 10.2 %collective-permute-start.5 = (f32[64,1024]{1,0:T(8,128)S(1)}, f32[64,1024]{1,0:T(8,128)S(1)}, u32[]{:S(2)}, u32[]{:S(2)}) collective-permute-start(f32[64,1024]{1,0:T(8,128)S(1)} %get-tuple-element.24), channel_id=1, source_target_pairs={{1,0},{2,1},{3,2},{5,4},{6,5},{7,6},{9,8},{10,9},{11,10},{13,12},{... | collective-permute-start | bytes 786440 | tf_op jit(solution)/shard_map/ppermute | solution.py:13
  377.2 9.1 %copy-start.3 = (f32[6,64,1024]{2,1,0:T(8,128)}, f32[6,64,1024]{2,1,0:T(8,128)S(1)}, u32[]{:S(2)}) copy-start(f32[6,64,1024]{2,1,0:T(8,128)S(1)} %slice.227) | copy-start | bytes 4718596
  478.8 11.1 %copy-start.4 = (f32[6,64,1024]{2,1,0:T(8,128)S(1)}, f32[6,64,1024]{2,1,0:T(8,128)}, u32[]{:S(2)}) copy-start(f32[6,64,1024]{2,1,0:T(8,128)} %copy-done.3) | copy-start | bytes 4718596
  493.8 9.5 %collective-permute-start.6 = (f32[64,1024]{1,0:T(8,128)S(1)}, f32[64,1024]{1,0:T(8,128)S(1)}, u32[]{:S(2)}, u32[]{:S(2)}) collective-permute-start(f32[64,1024]{1,0:T(8,128)S(1)} %get-tuple-element.19), channel_id=1, source_target_pairs={{0,1},{1,2},{2,3},{4,5},{5,6},{6,7},{8,9},{9,10},{10,11},{12,13},{... | collective-permute-start | bytes 786440 | tf_op jit(solution)/shard_map/ppermute | solution.py:13
  497.2 10.2 %collective-permute-start.7 = (f32[64,1024]{1,0:T(8,128)S(1)}, f32[64,1024]{1,0:T(8,128)S(1)}, u32[]{:S(2)}, u32[]{:S(2)}) collective-permute-start(f32[64,1024]{1,0:T(8,128)S(1)} %get-tuple-element.20), channel_id=1, source_target_pairs={{1,0},{2,1},{3,2},{5,4},{6,5},{7,6},{9,8},{10,9},{11,10},{13,12},{... | collective-permute-start | bytes 786440 | tf_op jit(solution)/shard_map/ppermute | solution.py:13
  (1 other events, 0.7 us)
Sparse Core Ops, SparseCore 0:
  20.0 56.6 all-reduce.4
  149.6 52.6 all-reduce.6
  275.5 52.6 all-reduce.8
  401.6 52.6 all-reduce.10
where the time goes:
time: 523 us; the launch traced here: 517 us
  waiting for transfers between devices  228 us (44%)
  other arithmetic  111 us (21%)
  blocking collectives  89.2 us (17%)
  matrix products  38.7 us (7%)
  starting transfers between devices  19.3 us (4%)
  local copies, waits for them, and re-layouts  16.6 us (3%)
  between operations  14.5 us (3%)
    psum x4, waiting for transfers between devices, local(): cross_sum, col_norms = lax.psum((cross_part, norm_part), 'row')  197 us
    psum x4, blocking collectives, local(): cross_sum, col_norms = lax.psum((cross_part, norm_part), 'row')  51.6 us
    another operation x13, other arithmetic, solve_systems(): factors = jnp.linalg.cholesky(systems)  49 us
    another operation x9, other arithmetic, solve_one(): return jax.scipy.linalg.cho_solve((factor, True), target)  42.4 us
    all_gather x4, blocking collectives, cayley_turn(): gathered = lax.all_gather(mine_solved, 'row', axis=0, tiled=True)  37.7 us
    ppermute x8, waiting for transfers between devices, shifted(): lax.ppermute(value, axis, [(source, source + steps) for source in range(l...  31.2 us
    ppermute x8, starting transfers between devices, shifted(): lax.ppermute(value, axis, [(source, source + steps) for source in range(l...  19 us
    dot_general x4, matrix products, local(): turned = jnp.einsum('pij,pim->pjm', turn_matrix, blocks, precision=highest)  15.6 us
  transfers between devices with their start and end apart: 12, of which 12 were waited for; matrix products, arithmetic and copies ran while one was open for 1% of the time, Pallas kernels for 0%

commit v1 on v0

v1 whole, which is shorter than its diff:
```python
import functools

import jax
import jax.numpy as jnp
from jax import lax
from jax.experimental import pallas as pl
from jax.experimental.pallas import tpu as pltpu
from jax.sharding import PartitionSpec as P

BLOCK = 64
PAIR = 2 * BLOCK
STEPS = 4
HALF = BLOCK // 2
PACKED = HALF + 8
UPPER = 1.0 + BLOCK * BLOCK * 0.0905
HIGHEST = lax.Precision.HIGHEST


def mm(a, b):
    return jnp.dot(a, b, precision=HIGHEST, preferred_element_type=jnp.float32)


def inverse(coupling, coupling_t, eye):
    system = eye + mm(coupling, coupling_t)
    low = 2.0 / (1.0 + UPPER)
    y = system * low
    reach = low * (2.0 - low)
    scale = 2.0 / (1.0 + reach)
    z = 2.0 * eye - y
    x = (scale * low) * z
    y = scale * mm(y, z)
    low = scale * reach
    while low < 0.99:
        z = 2.0 * eye - y
        reach = low * (2.0 - low)
        scale = 2.0 / (1.0 + reach)
        stacked = scale * mm(jnp.concatenate([x, y], axis=0), z)
        x, y = stacked[:BLOCK], stacked[BLOCK:]
        low = scale * reach
    x = x + mm(x, eye - mm(system, x))
    x = x + mm(x, eye - x - mm(coupling, mm(coupling_t, x)))
    return 0.5 * (x + x.T)


def turn_transposed(total):
    cross = jnp.concatenate([total[:HALF, :BLOCK], total[:HALF, BLOCK:]], axis=0)
    norms = total[HALF : HALF + 1, :]
    rows = lax.broadcasted_iota(jnp.int32, (BLOCK, BLOCK), 0)
    cols = lax.broadcasted_iota(jnp.int32, (BLOCK, BLOCK), 1)
    eye = jnp.where(rows == cols, 1.0, 0.0).astype(jnp.float32)
    top_norms = jnp.sum(jnp.where(rows == cols, norms[:, :BLOCK], 0.0), axis=1, keepdims=True)
    bottom_norms = norms[:, BLOCK:]
    spread = bottom_norms - top_norms
    square = spread * spread + 4.0 * cross * cross
    radius = jnp.sqrt(square)
    scale_term = (top_norms + bottom_norms) / BLOCK
    coupling = 2.0 * cross * spread / (square + jnp.abs(spread) * radius + scale_term * scale_term)
    coupling_t = coupling.T
    x = inverse(coupling, coupling_t, eye)
    lower = 2.0 * mm(coupling_t, x)
    upper = lower.T
    corner = eye - mm(lower, coupling)
    return jnp.concatenate(
        [jnp.concatenate([2.0 * x - eye, -upper], axis=1), jnp.concatenate([lower, corner], axis=1)], axis=0
    )


def kernel(rows, cols, pairs, order_ref, columns_ref, out_ref, x, grams, parts, turns, edges,
           gram_send, gram_recv, turn_send, turn_recv, pass_send, edge_send, edge_recv, out_sem):
    me = lax.axis_index("row")
    position = lax.axis_index("col")
    core = lax.rem(me, 2)
    chip = lax.div(me, 2)
    partner = me + 1 - 2 * core
    has_left = position > 0
    has_right = position < cols - 1
    last = pairs - 1
    width = pairs * PAIR

    barrier = pltpu.get_barrier_semaphore()

    def greet(other, carry):
        @pl.when(other != me)
        def _():
            pl.semaphore_signal(barrier, inc=1, device_id={"row": other})
        return carry

    lax.fori_loop(0, rows, greet, 0)

    @pl.when(has_left)
    def _():
        pl.semaphore_signal(barrier, inc=1, device_id={"col": position - 1})

    @pl.when(has_right)
    def _():
        pl.semaphore_signal(barrier, inc=1, device_id={"col": position + 1})

    def fill(slot, carry):
        source = lax.rem(order_ref[slot], 2 * pairs)
        x[0, pl.ds(pl.multiple_of(slot * BLOCK, BLOCK), BLOCK), :] = columns_ref[source]
        return carry

    lax.fori_loop(0, 2 * pairs, fill, 0)

    greeted = rows - 1 + has_left.astype(jnp.int32) + has_right.astype(jnp.int32)
    pl.semaphore_wait(barrier, greeted)

    def gram_copy(pair):
        return pltpu.make_async_remote_copy(
            src_ref=grams.at[pair], dst_ref=parts.at[me], send_sem=gram_send.at[pair], recv_sem=gram_recv.at[me],
            device_id={"row": pair},
        )

    def gram_arrival(source):
        return pltpu.make_async_remote_copy(
            src_ref=parts.at[source], dst_ref=parts.at[source], send_sem=gram_send.at[0],
            recv_sem=gram_recv.at[source], device_id={"row": partner},
        )

    def turn_copy(other):
        target = jnp.where(other == chip, partner, 2 * other + core)
        return pltpu.make_async_remote_copy(
            src_ref=turns.at[me], dst_ref=turns.at[me], send_sem=turn_send.at[other], recv_sem=turn_recv.at[me],
            device_id={"row": target},
        )

    def pass_copy(pair):
        return pltpu.make_async_remote_copy(
            src_ref=turns.at[pair], dst_ref=turns.at[pair], send_sem=pass_send.at[pair], recv_sem=turn_recv.at[pair],
            device_id={"row": partner},
        )

    def edge_left(after):
        return pltpu.make_async_remote_copy(
            src_ref=edges.at[0], dst_ref=x.at[after, pl.ds(last * PAIR + BLOCK, BLOCK)], send_sem=edge_send.at[0],
            recv_sem=edge_recv.at[after, 0], device_id={"col": position - 1},
        )

    def edge_right(after):
        return pltpu.make_async_remote_copy(
            src_ref=edges.at[1], dst_ref=x.at[after, pl.ds(0, BLOCK)], send_sem=edge_send.at[1],
            recv_sem=edge_recv.at[after, 1], device_id={"col": position + 1},
        )

    def wait_edges(now):
        @pl.when(has_left)
        def _():
            edge_right(now).wait_recv()

        @pl.when(has_right)
        def _():
            edge_left(now).wait_recv()

    def take_gram(pair, now):
        base = pl.multiple_of(pair * PAIR, PAIR)
        block = x[now, pl.ds(base, PAIR), :]
        cross = lax.dot_general(
            block[:BLOCK], block[BLOCK:], (((1,), (1,)), ((), ())), precision=HIGHEST,
            preferred_element_type=jnp.float32,
        )
        squares = block * block
        partial = squares[:, :128]
        for lane in range(1, squares.shape[1] // 128):
            partial = partial + squares[:, lane * 128 : (lane + 1) * 128]
        norms = jnp.sum(partial.T, axis=0, keepdims=True)
        grams[pair, :HALF, :] = jnp.concatenate([cross[:HALF], cross[HALF:]], axis=1)
        grams[pair, HALF:, :] = jnp.broadcast_to(norms, (8, PAIR))

        @pl.when(pair != me)
        def _():
            gram_copy(pair).start()

    def own():
        def gather(source, carry):
            @pl.when(source != me)
            def _():
                gram_arrival(source).wait_recv()
            return carry

        lax.fori_loop(0, rows, gather, 0)
        total = grams[me]
        for source in range(rows):
            total = total + jnp.where(source == me, 0.0, parts[source])
        turns[me] = turn_transposed(total)

        def spread_out(other, carry):
            turn_copy(other).start()
            return carry

        lax.fori_loop(0, rows // 2, spread_out, 0)

    def take_turn(pair):
        @pl.when(pair != me)
        def _():
            pass_copy(pair).wait_recv()

            @pl.when(lax.rem(pair, 2) == core)
            def _():
                pass_copy(pair).start()

    def apply(pair, now):
        base = pl.multiple_of(pair * PAIR, PAIR)
        return mm(turns[pair], x[now, pl.ds(base, PAIR), :])

    def step(index, carry):
        now = lax.rem(index, 2)
        after = 1 - now

        def inner_gram(pair, carry):
            take_gram(pair, now)
            return carry

        lax.fori_loop(1, last, inner_gram, 0)
        inner_owner = jnp.logical_and(me > 0, me < last)
        edge_owner = jnp.logical_or(me == 0, me == last)

        @pl.when(inner_owner)
        def _():
            own()

        @pl.when(index > 0)
        def _():
            wait_edges(now)

        def edge_gram(which, carry):
            take_gram(which * last, now)
            return carry

        lax.fori_loop(0, 2, edge_gram, 0)

        @pl.when(edge_owner)
        def _():
            own()

        def inner_apply(pair, carry):
            take_turn(pair)
            turned = apply(pair, now)
            x[after, pl.ds(pl.multiple_of((pair + 1) * PAIR, PAIR), BLOCK), :] = turned[:BLOCK]
            x[after, pl.ds(pl.multiple_of((pair - 1) * PAIR + BLOCK, BLOCK), BLOCK), :] = turned[BLOCK:]
            return carry

        lax.fori_loop(1, last, inner_apply, 0)

        @pl.when(jnp.logical_and(index > 0, has_left))
        def _():
            edge_left(after).wait_send()

        take_turn(0)
        turned = apply(0, now)
        x[after, pl.ds(pl.multiple_of(jnp.where(has_left, PAIR, 0), BLOCK), BLOCK), :] = turned[:BLOCK]

        @pl.when(has_left)
        def _():
            edges[0] = turned[BLOCK:]
            edge_left(after).start()

        @pl.when(jnp.logical_not(has_left))
        def _():
            x[after, pl.ds(PAIR, BLOCK), :] = turned[BLOCK:]

        @pl.when(jnp.logical_and(index > 0, has_right))
        def _():
            edge_right(after).wait_send()

        take_turn(last)
        turned_last = apply(last, now)
        x[after, pl.ds((last - 1) * PAIR + BLOCK, BLOCK), :] = turned_last[BLOCK:]

        @pl.when(has_right)
        def _():
            edges[1] = turned_last[:BLOCK]
            edge_right(after).start()

        @pl.when(jnp.logical_not(has_right))
        def _():
            x[after, pl.ds(last * PAIR + BLOCK, BLOCK), :] = turned_last[:BLOCK]

        def settle(pair, carry):
            @pl.when(pair != me)
            def _():
                gram_copy(pair).wait_send()

                @pl.when(lax.rem(pair, 2) == core)
                def _():
                    pass_copy(pair).wait_send()
            return carry

        lax.fori_loop(0, pairs, settle, 0)

        @pl.when(me < pairs)
        def _():
            def settle_turn(other, carry):
                turn_copy(other).wait_send()
                return carry

            lax.fori_loop(0, rows // 2, settle_turn, 0)

        return carry

    lax.fori_loop(0, STEPS, step, 0)
    final = STEPS % 2

    def out_copy(start, size, which):
        return pltpu.make_async_copy(
            x.at[final, pl.ds(start, size)], out_ref.at[pl.ds(start, size)], out_sem.at[which]
        )

    middle = out_copy(BLOCK, width - PAIR, 0)
    middle.start()
    wait_edges(final)
    first = out_copy(0, BLOCK, 1)
    first.start()
    ending = out_copy(width - BLOCK, BLOCK, 2)
    ending.start()

    @pl.when(has_left)
    def _():
        edge_left(final).wait_send()

    @pl.when(has_right)
    def _():
        edge_right(final).wait_send()

    middle.wait()
    first.wait()
    ending.wait()


def solution(mesh):
    rows, cols = mesh.shape["row"], mesh.shape["col"]

    def local(columns, block_order):
        width, length = columns.shape
        pairs = width // PAIR
        assert 3 <= pairs <= rows and rows % 2 == 0
        dma = pltpu.SemaphoreType.DMA
        return pl.pallas_call(
            functools.partial(kernel, rows, cols, pairs),
            out_shape=jax.ShapeDtypeStruct((width, length), jnp.float32),
            in_specs=[pl.BlockSpec(memory_space=pltpu.SMEM), pl.BlockSpec(memory_space=pltpu.VMEM)],
            out_specs=pl.BlockSpec(memory_space=pl.ANY),
            scratch_shapes=[
                pltpu.VMEM((2, width, length), jnp.float32),
                pltpu.VMEM((pairs, PACKED, PAIR), jnp.float32),
                pltpu.VMEM((rows, PACKED, PAIR), jnp.float32),
                pltpu.VMEM((pairs, PAIR, PAIR), jnp.float32),
                pltpu.VMEM((2, BLOCK, length), jnp.float32),
                dma((pairs,)),
                dma((rows,)),
                dma((rows // 2,)),
                dma((pairs,)),
                dma((pairs,)),
                dma((2,)),
                dma((2, 2)),
                dma((3,)),
            ],
            compiler_params=pltpu.CompilerParams(
                collective_id=0, has_side_effects=True, vmem_limit_bytes=56 * 1024 * 1024
            ),
        )(block_order, columns.reshape(2 * pairs, BLOCK, length))

    placed = (P("col", "row"), P("col"))
    return jax.shard_map(local, mesh=mesh, in_specs=placed, out_specs=P("col", "row"), check_vma=False)
```

time: 523 us -> 127 us (0.24); the launches traced: 517 us -> 127 us
  waiting for transfers between devices: 228 us -> 0 us
  Pallas kernels: 0 us -> 122 us
  other arithmetic: 111 us -> 0 us
  blocking collectives: 89.2 us -> 0 us
  matrix products: 38.7 us -> 0 us
  starting transfers between devices: 19.3 us -> 0 us
  between operations: 14.5 us -> 0.01 us
  local copies, waits for them, and re-layouts: 16.6 us -> 4.79 us
    psum x4 -> x0, waiting for transfers between devices: 197 us -> none  [local(): cross_sum, col_norms = lax.psum((cross_part, norm_part), 'row')]
    pallas_call x0 -> x1, Pallas kernels: none -> 122 us  [local(): pl.pallas_call(functools.partial(kernel, rows, cols, pairs), out_shape=ja...]
    another operation x22 -> x0, other arithmetic: 91.4 us -> none  [the longest x13 49 us: solve_systems(): factors = jnp.linalg.cholesky(systems)]
    psum x4 -> x0, blocking collectives: 51.6 us -> none  [local(): cross_sum, col_norms = lax.psum((cross_part, norm_part), 'row')]
    all_gather x4 -> x0, blocking collectives: 37.7 us -> none  [cayley_turn(): gathered = lax.all_gather(mine_solved, 'row', axis=0, tiled=True)]
    dot_general x20 -> x0, matrix products: 36.4 us -> none  [the longest x4 15.6 us: local(): turned = jnp.einsum('pij,pim->pjm', turn_matrix, blocks, precision=highest)]
    ppermute x8 -> x0, waiting for transfers between devices: 31.2 us -> none  [shifted(): lax.ppermute(value, axis, [(source, source + steps) for source in range(l...]
    ppermute x8 -> x0, starting transfers between devices: 19 us -> none  [shifted(): lax.ppermute(value, axis, [(source, source + steps) for source in range(l...]
  transfers between devices with their start and end apart: 12 -> 0, of which waited for: 12 -> 0; matrix products, arithmetic and copies ran while one was open for 1% -> 0% of each run, Pallas kernels for 0% -> 0%
where the time goes in v1:
time: 127 us
  Pallas kernels  122 us (96%)
  local copies, waits for them, and re-layouts  4.79 us (4%)
    pallas_call x1, Pallas kernels, local(): pl.pallas_call(functools.partial(kernel, rows, cols, pairs), out_shape=ja...  122 us
    unnamed x1, local copies, waits for them, and re-layouts  4.79 us

profile of v1, /device:TPU:0, one launch (start us, length us, event | category | flops | bytes accessed | tf_op | source)
XLA Modules:
  0.0 127.1 jit_solution(10750011523626597018)
XLA Ops:
  0.0 122.3 %shard_map.28 = f32[1024,1024]{1,0:T(8,128)} custom-call(s32[16]{0:T(128)} %order_ref.1, f32[16,64,1024]{2,1,0:T(8,128)} %bitcast.1), custom_call_target="tpu_custom_call" | custom-call | tf_op jit(solution)/shard_map/pallas_call | solution.py:337
  122.3 4.8 %copy.4 = f32[1024,1024]{1,0:T(8,128)} copy(f32[1024,1024]{1,0:T(8,128)} %shard_map.28) | data formatting | bytes 8388608

commit v2 on v1

--- a/solution.py
+++ b/solution.py
@@ -16,30 +16,57 @@
 HIGHEST = lax.Precision.HIGHEST
 
 
+def split(a):
+    high = a.astype(jnp.bfloat16)
+    rest = a - high.astype(jnp.float32)
+    middle = rest.astype(jnp.bfloat16)
+    return high, middle, (rest - middle.astype(jnp.float32)).astype(jnp.bfloat16)
+
+
+def chain(lefts, rights):
+    return jnp.dot(
+        jnp.concatenate(lefts, axis=1), jnp.concatenate(rights, axis=0), preferred_element_type=jnp.float32
+    )
+
+
+def mm3(a, b):
+    (ah, am, _), (bh, bm, _) = split(a), split(b)
+    return chain([ah, am, ah], [bh, bh, bm])
+
+
+def mm4(a, b):
+    (ah, am, al), (bh, bm, _) = split(a), split(b)
+    return chain([al, am, ah, ah], [bh, bh, bm, bh])
+
+
 def mm(a, b):
-    return jnp.dot(a, b, precision=HIGHEST, preferred_element_type=jnp.float32)
+    (ah, am, al), (bh, bm, bl) = split(a), split(b)
+    return chain([am, al, ah, ah, am, ah], [bm, bh, bl, bm, bh, bh])
 
 
 def inverse(coupling, coupling_t, eye):
-    system = eye + mm(coupling, coupling_t)
+    system = eye + mm3(coupling, coupling_t)
     low = 2.0 / (1.0 + UPPER)
     y = system * low
     reach = low * (2.0 - low)
     scale = 2.0 / (1.0 + reach)
     z = 2.0 * eye - y
     x = (scale * low) * z
-    y = scale * mm(y, z)
+    y = scale * mm3(y, z)
     low = scale * reach
     while low < 0.99:
         z = 2.0 * eye - y
         reach = low * (2.0 - low)
         scale = 2.0 / (1.0 + reach)
-        stacked = scale * mm(jnp.concatenate([x, y], axis=0), z)
+        stacked = scale * mm3(jnp.concatenate([x, y], axis=0), z)
         x, y = stacked[:BLOCK], stacked[BLOCK:]
         low = scale * reach
-    x = x + mm(x, eye - mm(system, x))
-    x = x + mm(x, eye - x - mm(coupling, mm(coupling_t, x)))
-    return 0.5 * (x + x.T)
+    x = x + mm3(x, eye - mm3(system, x))
+    product = mm(coupling_t, x)
+    residual = eye - x - mm(coupling, product)
+    stacked = jnp.concatenate([x, product], axis=0)
+    stacked = stacked + mm3(stacked, residual)
+    return stacked[:BLOCK], stacked[BLOCK:]
 
 
 def turn_transposed(total):
@@ -56,12 +83,28 @@
     scale_term = (top_norms + bottom_norms) / BLOCK
     coupling = 2.0 * cross * spread / (square + jnp.abs(spread) * radius + scale_term * scale_term)
     coupling_t = coupling.T
-    x = inverse(coupling, coupling_t, eye)
-    lower = 2.0 * mm(coupling_t, x)
-    upper = lower.T
+    x, product = inverse(coupling, coupling_t, eye)
+    lower = 2.0 * product
     corner = eye - mm(lower, coupling)
+    diagonal = jnp.sum(jnp.where(rows == cols, corner, 0.0), axis=0, keepdims=True)
+    mixed = jnp.where(rows <= cols, 2.0 * x - eye, corner)
+    body = jnp.concatenate([mixed, -lower.T], axis=1)
+    foot = jnp.broadcast_to(jnp.concatenate([diagonal, diagonal], axis=1), (8, PAIR))
+    return jnp.concatenate([body, foot], axis=0)
+
+
+def unpacked(packed):
+    rows = lax.broadcasted_iota(jnp.int32, (BLOCK, BLOCK), 0)
+    cols = lax.broadcasted_iota(jnp.int32, (BLOCK, BLOCK), 1)
+    mixed, upper = packed[:BLOCK, :BLOCK], packed[:BLOCK, BLOCK:]
+    flipped = mixed.T
+    corner = jnp.where(rows == cols, packed[BLOCK : BLOCK + 1, :BLOCK], jnp.where(rows > cols, mixed, flipped))
     return jnp.concatenate(
-        [jnp.concatenate([2.0 * x - eye, -upper], axis=1), jnp.concatenate([lower, corner], axis=1)], axis=0
+        [
+            jnp.concatenate([jnp.where(rows <= cols, mixed, flipped), upper], axis=1),
+            jnp.concatenate([-upper.T, corner], axis=1),
+        ],
+        axis=0,
     )
 
 
@@ -200,7 +243,7 @@
 
     def apply(pair, now):
         base = pl.multiple_of(pair * PAIR, PAIR)
-        return mm(turns[pair], x[now, pl.ds(base, PAIR), :])
+        return mm4(unpacked(turns[pair]), x[now, pl.ds(base, PAIR), :])
 
     def step(index, carry):
         now = lax.rem(index, 2)
@@ -211,13 +254,6 @@
             return carry
 
         lax.fori_loop(1, last, inner_gram, 0)
-        inner_owner = jnp.logical_and(me > 0, me < last)
-        edge_owner = jnp.logical_or(me == 0, me == last)
-
-        @pl.when(inner_owner)
-        def _():
-            own()
-
         @pl.when(index > 0)
         def _():
             wait_edges(now)
@@ -228,9 +264,43 @@
 
         lax.fori_loop(0, 2, edge_gram, 0)
 
-        @pl.when(edge_owner)
+        @pl.when(me < pairs)
         def _():
             own()
+
+        @pl.when(jnp.logical_and(index > 0, has_left))
+        def _():
+            edge_left(after).wait_send()
+
+        take_turn(0)
+        turned = apply(0, now)
+        x[after, pl.ds(pl.multiple_of(jnp.where(has_left, PAIR, 0), BLOCK), BLOCK), :] = turned[:BLOCK]
+
+        @pl.when(has_left)
+        def _():
+            edges[0] = turned[BLOCK:]
+            edge_left(after).start()
+
+        @pl.when(jnp.logical_not(has_left))
+        def _():
+            x[after, pl.ds(PAIR, BLOCK), :] = turned[BLOCK:]
+
+        @pl.when(jnp.logical_and(index > 0, has_right))
+        def _():
+            edge_right(after).wait_send()
+
+        take_turn(last)
+        turned_last = apply(last, now)
+        x[after, pl.ds((last - 1) * PAIR + BLOCK, BLOCK), :] = turned_last[BLOCK:]
+
+        @pl.when(has_right)
+        def _():
+            edges[1] = turned_last[:BLOCK]
+            edge_right(after).start()
+
+        @pl.when(jnp.logical_not(has_right))
+        def _():
+            x[after, pl.ds(last * PAIR + BLOCK, BLOCK), :] = turned_last[:BLOCK]
 
         def inner_apply(pair, carry):
             take_turn(pair)
@@ -240,40 +310,6 @@
             return carry
 
         lax.fori_loop(1, last, inner_apply, 0)
-
-        @pl.when(jnp.logical_and(index > 0, has_left))
-        def _():
-            edge_left(after).wait_send()
-
-        take_turn(0)
-        turned = apply(0, now)
-        x[after, pl.ds(pl.multiple_of(jnp.where(has_left, PAIR, 0), BLOCK), BLOCK), :] = turned[:BLOCK]
-
-        @pl.when(has_left)
-        def _():
-            edges[0] = turned[BLOCK:]
-            edge_left(after).start()
-
-        @pl.when(jnp.logical_not(has_left))
-        def _():
-            x[after, pl.ds(PAIR, BLOCK), :] = turned[BLOCK:]
-
-        @pl.when(jnp.logical_and(index > 0, has_right))
-        def _():
-            edge_right(after).wait_send()
-
-        take_turn(last)
-        turned_last = apply(last, now)
-        x[after, pl.ds((last - 1) * PAIR + BLOCK, BLOCK), :] = turned_last[BLOCK:]
-
-        @pl.when(has_right)
-        def _():
-            edges[1] = turned_last[:BLOCK]
-            edge_right(after).start()
-
-        @pl.when(jnp.logical_not(has_right))
-        def _():
-            x[after, pl.ds(last * PAIR + BLOCK, BLOCK), :] = turned_last[:BLOCK]
 
         def settle(pair, carry):
             @pl.when(pair != me)
@@ -343,7 +379,7 @@
                 pltpu.VMEM((2, width, length), jnp.float32),
                 pltpu.VMEM((pairs, PACKED, PAIR), jnp.float32),
                 pltpu.VMEM((rows, PACKED, PAIR), jnp.float32),
-                pltpu.VMEM((pairs, PAIR, PAIR), jnp.float32),
+                pltpu.VMEM((pairs, BLOCK + 8, PAIR), jnp.float32),
                 pltpu.VMEM((2, BLOCK, length), jnp.float32),
                 dma((pairs,)),
                 dma((rows,)),

time: 127 us -> 101 us (0.80); the launches traced: 127 us -> 99.7 us
  Pallas kernels: 122 us -> 94.9 us
    pallas_call x1, Pallas kernels: 122 us -> 94.9 us  [local(): pl.pallas_call(functools.partial(kernel, rows, cols, pairs), out_shape=ja...]
where the time goes in v2:
time: 101 us; the launch traced here: 99.7 us
  Pallas kernels  94.9 us (94%)
  local copies, waits for them, and re-layouts  4.79 us (5%)
    pallas_call x1, Pallas kernels, local(): pl.pallas_call(functools.partial(kernel, rows, cols, pairs), out_shape=ja...  94.9 us
    unnamed x1, local copies, waits for them, and re-layouts  4.79 us

profile of v2, /device:TPU:0, one launch (start us, length us, event | category | flops | bytes accessed | tf_op | source)
XLA Modules:
  0.0 99.7 jit_solution(13647535191169778777)
XLA Ops:
  0.0 94.9 %shard_map.28 = f32[1024,1024]{1,0:T(8,128)} custom-call(s32[16]{0:T(128)} %order_ref.1, f32[16,64,1024]{2,1,0:T(8,128)} %bitcast.1), custom_call_target="tpu_custom_call" | custom-call | tf_op jit(solution)/shard_map/pallas_call | solution.py:373
  94.9 4.8 %copy.4 = f32[1024,1024]{1,0:T(8,128)} copy(f32[1024,1024]{1,0:T(8,128)} %shard_map.28) | data formatting | bytes 8388608
